TPU v7x, 256 devices: a whole 4x4x8 slice. The times are simulated.
256 devices in a mesh: fsdp: 32 (over y, x, z_lo), rep: 8 (over z_hi, core).
Axes of the slice: x: 4, y: 4, z: 8 (z_hi: 4, z_lo: 2; z = z_hi * 2 + z_lo), core: 2. Of those that a mesh axis runs over, the one named last changes fastest.
Arguments:
- tokens: bfloat16 [122880, 3584], P(('fsdp', 'rep')), may hold values from -6 to 6
- positions: int32 [122880], P(('fsdp', 'rep')), may hold values from 0 to 4095
- slow_weight: float32 [3584, 4096], P('fsdp', 'rep'), may hold values from -0.09375 to 0.09375
- fast_weight: bfloat16 [8, 3584, 4096], P('rep', 'fsdp'), may hold values from -0.125 to 0.125
- slow_gain: float32 [3584], P(('fsdp', 'rep')), may hold values from -3 to 3
- fast_gain: bfloat16 [8, 3584], P('rep', 'fsdp'), may hold values from -3 to 3
Outputs:
- query_states: bfloat16 [122880, 2048], P(('fsdp', 'rep'))
- key_states: bfloat16 [122880, 1024], P(('fsdp', 'rep'))
- value_states: bfloat16 [122880, 1024], P(('fsdp', 'rep'))
- new_weight: float32 [3584, 4096], P('fsdp', 'rep')
- new_gain: float32 [3584], P(('fsdp', 'rep'))
All inputs are finite; a program needn't handle non-finite values.
Results may differ from a plain program's by a relative error of at most 0.012.
Values may be sent and summed in bfloat16 or wider, within the bound.
A program may use at most 128 MiB of HBM per device.

v0:
```python
import jax
import jax.numpy as jnp
from jax import lax
from jax.sharding import PartitionSpec as P

QHEADS = 8
KVHEADS = 4
HEAD = 256
EPSILON = 1e-06
ADVANCE_RATE = 0.5
ROPE_BASE = 10000.0


def cut_along(x, dim, devices):
    lengths = x.shape
    tiles = x.reshape(*lengths[:dim], devices, lengths[dim] // devices, *lengths[dim + 1 :])
    return jnp.moveaxis(tiles, dim, 0)


def one_scatter(arrays, axis, dims):
    devices = lax.axis_size(axis)
    tiles = [cut_along(a, dim, devices) for a, dim in zip(arrays, dims)]
    lines = jnp.concatenate([b.reshape(devices, -1) for b in tiles], axis=1)
    width = max(16, -(-lines.shape[1] // 1024) * 8)
    lines = jnp.pad(lines, ((0, 0), (0, width * 128 - lines.shape[1]))).reshape(-1, 128)
    line, at, done = (lax.psum_scatter(lines, axis, tiled=True).reshape(-1), 0, [])
    for b in tiles:
        part = b[0]
        done.append(line[at : at + part.size].reshape(part.shape))
        at += part.size
    return tuple(done)


def rotate(values, positions, head_count):
    row_count = values.shape[0]
    head_width = values.shape[1] // head_count
    half_width = head_width // 2
    by_head = values.reshape(row_count, head_count, head_width)
    inverse_rates = ROPE_BASE ** (-(jnp.arange(half_width, dtype=jnp.float32) * 2.0 / head_width))
    angles = positions.astype(jnp.float32)[:, None] * inverse_rates[None, :]
    cosine_table = jnp.cos(angles)[:, None, :]
    sine_table = jnp.sin(angles)[:, None, :]
    front_half = by_head[:, :, :half_width]
    back_half = by_head[:, :, half_width:]
    turned = jnp.concatenate(
        [
            front_half * cosine_table - back_half * sine_table,
            back_half * cosine_table + front_half * sine_table,
        ],
        axis=2,
    )
    return turned.reshape(row_count, head_count * head_width)


def on_device(tokens, positions, slow_weight, fast_weight, slow_gain, fast_gain):
    replicas = lax.axis_size("rep")
    totals = tuple(
        (
            part.astype(jnp.float32)
            for part in one_scatter(
                (
                    fast_weight.astype(jnp.float32).astype(jnp.bfloat16),
                    fast_gain.astype(jnp.float32).astype(jnp.bfloat16),
                ),
                "rep",
                (2, 1),
            )
        )
    )
    new_weight = slow_weight + ADVANCE_RATE * (totals[0][0] / replicas - slow_weight)
    new_gain = slow_gain + ADVANCE_RATE * (totals[1][0] / replicas - slow_gain)
    own_weight = new_weight.astype(jnp.bfloat16)
    own_gain = new_gain.astype(jnp.bfloat16)
    floats = tokens.astype(jnp.float32)
    inv_rms = lax.rsqrt(jnp.mean(floats * floats, axis=1, keepdims=True) + EPSILON)
    column_weight = lax.all_gather(own_weight, "fsdp", axis=0, tiled=True)
    whole_gain = lax.all_gather(own_gain, ("fsdp", "rep"), axis=0, tiled=True)
    normed = (floats * inv_rms * (1.0 + whole_gain.astype(jnp.float32))[None, :]).astype(
        jnp.bfloat16
    )
    projected = jnp.dot(
        normed,
        lax.all_gather(column_weight, "rep", axis=1, tiled=True),
        preferred_element_type=jnp.float32,
    )
    query_cols = QHEADS * HEAD
    key_cols = KVHEADS * HEAD
    query_states = rotate(projected[:, :query_cols], positions, QHEADS).astype(jnp.bfloat16)
    key_states = rotate(
        projected[:, query_cols : query_cols + key_cols], positions, KVHEADS
    ).astype(jnp.bfloat16)
    value_states = projected[:, query_cols + key_cols :].astype(jnp.bfloat16)
    return (query_states, key_states, value_states, new_weight, new_gain)


def solution(mesh):
    return jax.shard_map(
        on_device,
        mesh=mesh,
        in_specs=(
            P(("fsdp", "rep"), None),
            P(("fsdp", "rep")),
            P("fsdp", "rep"),
            P("rep", "fsdp", None),
            P(("fsdp", "rep")),
            P("rep", "fsdp"),
        ),
        out_specs=(
            P(("fsdp", "rep"), None),
            P(("fsdp", "rep"), None),
            P(("fsdp", "rep"), None),
            P("fsdp", "rep"),
            P(("fsdp", "rep")),
        ),
        check_vma=False,
    )
```

profile of v0, /device:TPU:35, one launch (start us, length us, event | category | flops | bytes accessed | tf_op | source)
XLA Modules:
  0.0 565.5 jit_solution(11715870747473245055)
XLA Ops:
  7.2 1.5 copy.11
  8.7 0.5 broadcast.84
  9.2 1.3 reduce.3
  10.6 0.1 reshape_transpose_reshape.3
  10.7 0.1 fusion.9
  10.7 1.4 reshape.107
  12.1 0.0 all-gather.3.cloned.1.call-start
  12.2 0.6 dynamic-slice
  13.8 75.9 %all-reduce.5.cloned.1.call-done = bf16[3648,128]{1,0:T(8,128)(2,1)} async-done(((bf16[3648,128]{1,0:T(8,128)(2,1)}), bf16[3648,128]{1,0:T(8,128)(2,1)}) %all-reduce.5.cloned.1.call-update) | async-done | bytes 933904
  89.7 1.6 convert_multiply_fusion.2
  91.3 1.7 div.28
  92.9 1.8 fusion.13
  94.8 141.0 %all-gather.3.cloned.1.call-done = bf16[3584,512]{1,0:T(8,128)(2,1)} async-done(((bf16[112,512]{1,0:T(8,128)(2,1)}), bf16[3584,512]{1,0:T(8,128)(2,1)}) %all-gather.3.cloned.1.call-update) | async-done | bytes 3670032 | tf_op jit(solution)/shard_map/all_gather | solution.py:76
  235.9 0.7 fusion
  236.6 1.7 multiply_cosine_fusion
  238.3 0.9 dynamic-slice_bitcast_fusion
  239.2 0.5 fusion.12
  239.8 0.2 dynamic-update-slice
  239.9 109.2 %all-reduce.1 = bf16[3584]{0:T(1024)(128)(2,1)S(1)} all-reduce(bf16[3584]{0:T(1024)(128)(2,1)S(1)} %dynamic-update-slice), channel_id=1, replica_groups=mesh['fsdp'=32,'rep'=8] {'fsdp','rep'}, use_global_device_ids=true, to_apply=%add.1 | all-reduce | flops 3584 | bytes 14336
  349.2 176.8 %all-gather.5.cloned.1.call-done = bf16[3584,4096]{1,0:T(8,128)(2,1)} async-done(((bf16[3584,512]{1,0:T(8,128)(2,1)}), bf16[3584,4096]{1,0:T(8,128)(2,1)}) %all-gather.5.cloned.1.call-update) | async-done | bytes 29360144 | tf_op jit(solution)/shard_map/all_gather | solution.py:83
  526.0 19.2 %fusion.3 = f32[480,4096]{1,0:T(8,128)S(1)} fusion(bf16[3584,4096]{1,0:T(8,128)(2,1)} %all-gather.5.cloned.1.call-done, bf16[480,3584]{1,0:T(8,128)(2,1)} %param.6, f32[3584]{0:T(1024)S(1)} %convert_add_fusion, f32[480]{0:T(512)S(1)} %add_rsqrt_fusion), kind=kOutput, calls=%fused_computation.5 | convolution fusion | flops 14099742720 | bytes 40681344 | tf_op jit(solution)/shard_map/dot_general | solution.py:81
  545.2 1.5 slice.42
  546.7 2.1 copy-done
  548.9 1.1 slice.62
  550.0 2.2 reshape.110
  552.2 0.5 subtract_convert_fusion.1
  552.7 0.5 pad_maximum_fusion.1
  553.3 1.1 copy.14
  554.4 1.8 copy.12
  556.2 0.6 subtract_convert_fusion
  556.9 0.2 pad_maximum_fusion
  557.1 1.9 copy.13
  (23 shorter events, 0.2 us)
Async XLA Ops:
  7.2 5.0 copy-start.5
  7.2 82.5 %all-reduce.5.cloned.1.call-start = ((), (), s32[]{:S(2)}) async-start(), calls=%async_computation.2 | async-start | bytes 1867776
  12.1 223.7 %copy-start.3 = (s32[480]{0:T(512)S(1)}, s32[480]{0:T(512)}, u32[]{:S(2)}) copy-start(s32[480]{0:T(512)} %param.7) | copy-start | bytes 5764
  12.1 223.8 %copy-start.1 = (bf16[480,3584]{1,0:T(8,128)(2,1)S(1)}, bf16[480,3584]{1,0:T(8,128)(2,1)}, u32[]{:S(2)}) copy-start(bf16[480,3584]{1,0:T(8,128)(2,1)} %param.6) | copy-start | bytes 10321924
  12.1 223.7 %all-gather.3.cloned.1.call-start = ((), (), s32[]{:S(2)}) async-start(), calls=%async_computation | async-start | bytes 3784704 | tf_op jit(solution)/shard_map/all_gather | solution.py:76
  94.8 431.2 %all-gather.5.cloned.1.call-start = ((), (), s32[]{:S(2)}) async-start(), calls=%async_computation.1 | async-start | bytes 33030144 | tf_op jit(solution)/shard_map/all_gather | solution.py:83
  235.8 3.5 copy-start.4
  545.2 3.7 copy-start
  550.0 2.2 copy-start.2
  552.2 2.2 slice-start
Sparse Core Ops, SparseCore 0:
  12.2 77.4 all-reduce.4
  94.9 140.8 all-gather.2
  237.6 288.3 all-gather.4
where the time goes:
time: 566 us
  waiting for transfers between devices  394 us (70%)
  blocking collectives  109 us (19%)
  matrix products  19.2 us (3%)
  local copies, waits for them, and re-layouts  18.6 us (3%)
  between operations  14.9 us (3%)
  other arithmetic  9.67 us (2%)
    all_gather x1, waiting for transfers between devices, on_device(): lax.all_gather(column_weight, 'rep', axis=1, tiled=True)  177 us
    all_gather x1, waiting for transfers between devices, on_device(): column_weight = lax.all_gather(own_weight, 'fsdp', axis=0, tiled=True)  141 us
    unnamed x1, blocking collectives  109 us
    unnamed x4, waiting for transfers between devices  76 us
    dot_general x1, matrix products, on_device(): jnp.dot(normed, lax.all_gather(column_weight, 'rep', axis=1, tiled=True),...  19.2 us
  transfers between devices with their start and end apart: 3, of which 3 were waited for; matrix products, arithmetic and copies ran while one was open for 1% of the time, Pallas kernels for 0%

commit v1 on v0

--- a/solution.py
+++ b/solution.py
@@ -80,7 +80,7 @@
     )
     projected = jnp.dot(
         normed,
-        lax.all_gather(column_weight, "rep", axis=1, tiled=True),
+        jnp.concatenate(lax.all_gather(column_weight, "rep"), axis=1),
         preferred_element_type=jnp.float32,
     )
     query_cols = QHEADS * HEAD

time: 566 us -> 607 us (1.072)
  local copies, waits for them, and re-layouts: 18.6 us -> 54.6 us
    reshape x0 -> x1, local copies, waits for them, and re-layouts: none -> 36 us  [on_device(): jnp.concatenate(lax.all_gather(column_weight, 'rep'), axis=1)]
where the time goes in v1:
time: 607 us; the launch traced here: 606 us
  waiting for transfers between devices  392 us (65%)
  blocking collectives  111 us (18%)
  local copies, waits for them, and re-layouts  54.6 us (9%)
  matrix products  21.9 us (4%)
  between operations  14.9 us (2%)
  other arithmetic  11.1 us (2%)
    all_gather x1, waiting for transfers between devices, on_device(): lax.all_gather(column_weight, 'rep')  175 us
    all_gather x1, waiting for transfers between devices, on_device(): column_weight = lax.all_gather(own_weight, 'fsdp', axis=0, tiled=True)  141 us
    unnamed x1, blocking collectives  111 us
    unnamed x4, waiting for transfers between devices  76 us
    reshape x1, local copies, waits for them, and re-layouts, on_device(): jnp.concatenate(lax.all_gather(column_weight, 'rep'), axis=1)  36 us
    dot_general x1, matrix products, on_device(): jnp.dot(normed, jnp.concatenate(lax.all_gather(column_weight, 'rep'), axi...  21.9 us
  transfers between devices with their start and end apart: 3, of which 3 were waited for; matrix products, arithmetic and copies ran while one was open for 1% of the time, Pallas kernels for 0%

profile of v1, /device:TPU:35, one launch (start us, length us, event | category | flops | bytes accessed | tf_op | source)
XLA Modules:
  0.0 605.6 jit_solution(3037273100259408362)
XLA Ops:
  7.2 0.5 broadcast.84
  7.7 1.3 reduce.3
  9.1 0.1 reshape_transpose_reshape.3
  9.1 1.5 copy.13
  10.7 0.1 fusion.9
  10.7 1.4 reshape.113
  12.1 0.0 all-gather.4.cloned.1.call-start
  12.2 0.6 dynamic-slice
  13.8 75.9 %all-reduce.5.cloned.1.call-done = bf16[3648,128]{1,0:T(8,128)(2,1)} async-done(((bf16[3648,128]{1,0:T(8,128)(2,1)}), bf16[3648,128]{1,0:T(8,128)(2,1)}) %all-reduce.5.cloned.1.call-update) | async-done | bytes 933904
  89.7 1.6 convert_multiply_fusion.2
  91.3 1.7 div.28
  92.9 1.8 fusion.13
  94.8 141.0 %all-gather.4.cloned.1.call-done = bf16[3584,512]{1,0:T(8,128)(2,1)} async-done(((bf16[112,512]{1,0:T(8,128)(2,1)}), bf16[3584,512]{1,0:T(8,128)(2,1)}) %all-gather.4.cloned.1.call-update) | async-done | bytes 3670032 | tf_op jit(solution)/shard_map/all_gather | solution.py:76
  235.9 0.7 fusion
  236.6 1.7 multiply_cosine_fusion
  238.4 0.9 dynamic-slice_bitcast_fusion
  239.3 0.5 fusion.12
  239.8 0.2 dynamic-update-slice
  240.0 110.7 %all-reduce.1 = bf16[3584]{0:T(1024)(128)(2,1)S(1)} all-reduce(bf16[3584]{0:T(1024)(128)(2,1)S(1)} %dynamic-update-slice), channel_id=1, replica_groups=mesh['fsdp'=32,'rep'=8] {'fsdp','rep'}, use_global_device_ids=true, to_apply=%add.1 | all-reduce | flops 3584 | bytes 14336
  350.7 175.3 %all-gather.6.cloned.1.call-done = bf16[28672,512]{1,0:T(8,128)(2,1)} async-done(((bf16[3584,512]{1,0:T(8,128)(2,1)}), bf16[28672,512]{1,0:T(8,128)(2,1)}) %all-gather.6.cloned.1.call-update) | async-done | bytes 29360144 | tf_op jit(solution)/shard_map/all_gather | solution.py:83
  526.0 36.0 %copy.12 = bf16[3584,8,512]{0,2,1:T(8,128)(2,1)} copy(bf16[3584,8,512]{2,0,1:T(8,128)(2,1)} %bitcast.22) | data formatting | bytes 58720256 | tf_op jit(solution)/shard_map/reshape | solution.py:83
  562.0 21.9 %fusion.3 = f32[480,4096]{1,0:T(8,128)} fusion(bf16[3584,4096]{0,1:T(8,128)(2,1)} %bitcast.23, bf16[480,3584]{1,0:T(8,128)(2,1)S(1)} %copy-done, f32[3584]{0:T(1024)S(1)} %convert_add_fusion, f32[480]{0:T(512)S(1)} %add_rsqrt_fusion), kind=kOutput, calls=%fused_computation.5 | convolution fusion | flops 14099742720 | bytes 40681344 | tf_op jit(solution)/shard_map/dot_general | solution.py:81
  584.0 2.6 slice.62
  586.6 2.1 slice-done.1
  588.7 1.8 copy.14
  590.6 0.5 subtract_convert_fusion
  591.1 0.2 pad_maximum_fusion
  591.3 1.9 copy.15
  593.2 2.2 reshape.118
  595.4 2.0 subtract_convert_fusion.1
  597.4 0.5 pad_maximum_fusion.1
  597.9 1.1 copy.16
  (25 shorter events, 0.2 us)
Async XLA Ops:
  7.2 5.0 copy-start.5
  7.2 82.5 %all-reduce.5.cloned.1.call-start = ((), (), s32[]{:S(2)}) async-start(), calls=%async_computation.2 | async-start | bytes 1867776
  12.1 223.7 %copy-start.3 = (s32[480]{0:T(512)S(1)}, s32[480]{0:T(512)}, u32[]{:S(2)}) copy-start(s32[480]{0:T(512)} %param.7) | copy-start | bytes 5764
  12.1 223.8 %copy-start = (bf16[480,3584]{1,0:T(8,128)(2,1)S(1)}, bf16[480,3584]{1,0:T(8,128)(2,1)}, u32[]{:S(2)}) copy-start(bf16[480,3584]{1,0:T(8,128)(2,1)} %param.6) | copy-start | bytes 10321924
  12.1 223.7 %all-gather.4.cloned.1.call-start = ((), (), s32[]{:S(2)}) async-start(), calls=%async_computation | async-start | bytes 3784704 | tf_op jit(solution)/shard_map/all_gather | solution.py:76
  94.8 431.2 %all-gather.6.cloned.1.call-start = ((), (), s32[]{:S(2)}) async-start(), calls=%async_computation.1 | async-start | bytes 33030144 | tf_op jit(solution)/shard_map/all_gather | solution.py:83
  235.8 3.5 copy-start.4
  586.6 2.1 slice-start.1
  588.7 1.8 copy-start.1
  588.7 1.8 copy-start.2
  591.1 2.1 slice-start
Sparse Core Ops, SparseCore 0:
  12.2 77.4 all-reduce.4
  94.9 140.8 all-gather.3
  237.6 288.3 all-gather.5

commit v2 on v0

--- a/solution.py
+++ b/solution.py
@@ -73,7 +73,9 @@
     own_gain = new_gain.astype(jnp.bfloat16)
     floats = tokens.astype(jnp.float32)
     inv_rms = lax.rsqrt(jnp.mean(floats * floats, axis=1, keepdims=True) + EPSILON)
-    column_weight = lax.all_gather(own_weight, "fsdp", axis=0, tiled=True)
+    column_weight = jnp.concatenate(
+        lax.all_to_all(jnp.stack([own_weight] * lax.axis_size("fsdp")), "fsdp", 0, 0), axis=0
+    )
     whole_gain = lax.all_gather(own_gain, ("fsdp", "rep"), axis=0, tiled=True)
     normed = (floats * inv_rms * (1.0 + whole_gain.astype(jnp.float32))[None, :]).astype(
         jnp.bfloat16

time: 566 us -> 447 us (0.79)
  waiting for transfers between devices: 394 us -> 246 us
  blocking collectives: 109 us -> 139 us
    all_gather x1 -> x0, waiting for transfers between devices: 141 us -> none  [on_device(): column_weight = lax.all_gather(own_weight, 'fsdp', axis=0, tiled=True)]
    all_to_all x0 -> x1, blocking collectives: none -> 49.9 us  [on_device(): lax.all_to_all(jnp.stack([own_weight] * lax.axis_size('fsdp')), 'fsdp', 0...]
    unnamed x1, blocking collectives: 109 us -> 89.3 us
    all_gather x1, waiting for transfers between devices: 177 us -> 170 us  [on_device(): lax.all_gather(column_weight, 'rep', axis=1, tiled=True)]
    unnamed x20 -> x22, local copies, waits for them, and re-layouts: 9.83 us -> 11.8 us
    unnamed x4 -> x3, waiting for transfers between devices: 76 us -> 76.3 us
  transfers between devices with their start and end apart: 3 -> 2, of which waited for: 3 -> 2; matrix products, arithmetic and copies ran while one was open for 1% -> 1% of each run, Pallas kernels for 0% -> 0%
where the time goes in v2:
time: 447 us
  waiting for transfers between devices  246 us (55%)
  blocking collectives  139 us (31%)
  local copies, waits for them, and re-layouts  19.4 us (4%)
  matrix products  19.2 us (4%)
  between operations  14.8 us (3%)
  other arithmetic  7.9 us (2%)
    all_gather x1, waiting for transfers between devices, on_device(): lax.all_gather(column_weight, 'rep', axis=1, tiled=True)  170 us
    unnamed x1, blocking collectives  89.3 us
    unnamed x3, waiting for transfers between devices  76.3 us
    all_to_all x1, blocking collectives, on_device(): lax.all_to_all(jnp.stack([own_weight] * lax.axis_size('fsdp')), 'fsdp', 0...  49.9 us
    dot_general x1, matrix products, on_device(): jnp.dot(normed, lax.all_gather(column_weight, 'rep', axis=1, tiled=True),...  19.2 us
    unnamed x22, local copies, waits for them, and re-layouts  11.8 us
  transfers between devices with their start and end apart: 2, of which 2 were waited for; matrix products, arithmetic and copies ran while one was open for 1% of the time, Pallas kernels for 0%

profile of v2, /device:TPU:35, one launch (start us, length us, event | category | flops | bytes accessed | tf_op | source)
XLA Modules:
  0.0 446.7 jit_solution(7679281555094527782)
XLA Ops:
  7.2 1.5 copy.11
  8.8 0.5 broadcast.86
  9.3 1.3 reduce.3
  10.6 0.1 reshape_transpose_reshape.3
  10.8 1.4 reshape.112
  12.2 0.6 dynamic-slice
  13.5 76.3 %all-reduce.5.cloned.1.call-done = bf16[3648,128]{1,0:T(8,128)(2,1)} async-done(((bf16[3648,128]{1,0:T(8,128)(2,1)}), bf16[3648,128]{1,0:T(8,128)(2,1)}) %all-reduce.5.cloned.1.call-update) | async-done | bytes 933904
  89.7 0.9 convert_multiply_fusion.2
  90.7 0.7 fusion.13
  91.4 0.4 stack.2
  91.8 49.9 %all_to_all.5 = bf16[32,112,512]{2,1,0:T(8,128)(2,1)} all-to-all(bf16[32,112,512]{2,1,0:T(8,128)(2,1)S(1)} %stack.2), channel_id=1, replica_groups=mesh['fsdp'=32,'rep'=8] {'fsdp'}, dimensions={0} | all-to-all | bytes 7340032 | tf_op jit(solution)/shard_map/all_to_all | solution.py:77
  141.8 0.6 copy-done.4
  142.4 1.3 copy-done.1
  143.7 0.7 fusion
  144.5 1.7 multiply_cosine_fusion
  146.2 0.9 dynamic-slice_bitcast_fusion
  147.1 0.5 fusion.12
  147.6 0.2 dynamic-update-slice
  147.8 89.3 %all-reduce.1 = bf16[3584]{0:T(1024)(128)(2,1)S(1)} all-reduce(bf16[3584]{0:T(1024)(128)(2,1)S(1)} %dynamic-update-slice), channel_id=1, replica_groups=mesh['fsdp'=32,'rep'=8] {'fsdp','rep'}, use_global_device_ids=true, to_apply=%add.1 | all-reduce | flops 3584 | bytes 14336
  237.1 169.8 %all-gather.2.cloned.1.call-done = bf16[3584,4096]{1,0:T(8,128)(2,1)} async-done(((bf16[3584,512]{1,0:T(8,128)(2,1)}), bf16[3584,4096]{1,0:T(8,128)(2,1)}) %all-gather.2.cloned.1.call-update) | async-done | bytes 29360144 | tf_op jit(solution)/shard_map/all_gather | solution.py:85
  406.9 19.2 %fusion.3 = f32[480,4096]{1,0:T(8,128)S(1)} fusion(bf16[3584,4096]{1,0:T(8,128)(2,1)} %all-gather.2.cloned.1.call-done, bf16[480,3584]{1,0:T(8,128)(2,1)} %param.6, f32[3584]{0:T(1024)S(1)} %convert_add_fusion, f32[480]{0:T(512)S(1)} %add_rsqrt_fusion), kind=kOutput, calls=%fused_computation.5 | convolution fusion | flops 14099742720 | bytes 40681344 | tf_op jit(solution)/shard_map/dot_general | solution.py:83
  426.1 1.5 slice.42
  427.6 2.1 copy-done
  429.7 1.1 slice.62
  430.8 2.2 reshape.116
  433.0 0.5 subtract_convert_fusion.1
  433.6 0.5 pad_maximum_fusion.1
  434.1 1.1 copy.14
  435.3 1.8 copy.12
  437.1 0.6 subtract_convert_fusion
  437.7 0.2 pad_maximum_fusion
  437.9 1.9 copy.13
  (24 shorter events, 0.3 us)
Async XLA Ops:
  7.2 5.0 %copy-start.6 = (u32[256]{0:T(256)S(1)}, u32[256]{0:T(256)}, u32[]{:S(2)}) copy-start(u32[256]{0:T(256)} %constant.41) | copy-start | bytes 3076
  7.2 82.5 %all-reduce.5.cloned.1.call-start = ((), (), s32[]{:S(2)}) async-start(), calls=%async_computation.2 | async-start | bytes 1867776
  7.2 83.5 %copy-start.3 = (f32[112,512]{1,0:T(8,128)S(1)}, f32[112,512]{1,0:T(8,128)}, u32[]{:S(2)}) copy-start(f32[112,512]{1,0:T(8,128)} %param.8) | copy-start | bytes 688132
  12.2 394.7 %all-gather.2.cloned.1.call-start = ((), (), s32[]{:S(2)}) async-start(), calls=%async_computation.1 | async-start | bytes 33030144 | tf_op jit(solution)/shard_map/all_gather | solution.py:85
  141.7 0.7 copy-start.4
  141.7 2.0 copy-start.1
  141.7 5.4 %copy-start.5 = (f32[14]{0:T(128)S(1)}, f32[14]{0:T(128)}, u32[]{:S(2)}) copy-start(f32[14]{0:T(128)} %param.10) | copy-start | bytes 172
  426.1 3.6 copy-start
  430.8 2.2 copy-start.2
  433.0 2.2 slice-start
Sparse Core Ops, SparseCore 0:
  12.3 77.4 all-reduce.4
  141.9 264.9 all-gather.1
